TPU v7x, 32 devices: a whole 2x2x4 slice. The times are simulated.
32 devices in a mesh: gx: 4 (over y, x), gy: 2 (over core), gz: 4 (over z).
Axes of the slice: x: 2, y: 2, z: 4, core: 2. Of those that a mesh axis runs over, the one named last changes fastest.
Arguments:
- initial: float32 [256, 64, 1024], P('gx', 'gy', 'gz'), may hold values from -6 to 6
- right_side: float32 [256, 64, 1024], P('gx', 'gy', 'gz'), may hold values from -12 to 12
- shift_field: float32 [256, 64, 1024], P('gx', 'gy', 'gz'), may hold values from 0.5 to 8
Outputs:
- relaxed: float32 [256, 64, 1024], P('gx', 'gy', 'gz')
All inputs are finite; a program needn't handle non-finite values.
Results may differ from a plain program's by a relative error of at most 0.00002.
Values sent between devices are 32-bit elements; how exact they have to be, the bound alone decides.
A program may use at most 128 MiB of HBM per device.

v0:
```python
import jax
import jax.numpy as jnp
from jax import lax
from jax.sharding import PartitionSpec as P

SWEEPS = 4


relax_weight = 0.8


def extended(cells, sides, width):
    for axis, dim in sides:
        count = lax.axis_size(axis)
        head = lax.slice_in_dim(cells, 0, width, axis=dim)
        tail = lax.slice_in_dim(cells, cells.shape[dim] - width, cells.shape[dim], axis=dim)
        cells = jnp.concatenate(
            [
                lax.ppermute(tail, axis, [(i, (i + 1) % count) for i in range(count)]),
                cells,
                lax.ppermute(head, axis, [((i + 1) % count, i) for i in range(count)]),
            ],
            axis=dim,
        )
    return cells


def relax_margin(field, rhs_ext, shift_ext):
    centre = field[1:-1, 1:-1, 1:-1]
    beside = field[2:, 1:-1, 1:-1] + field[:-2, 1:-1, 1:-1]
    beside = beside + field[1:-1, 2:, 1:-1] + field[1:-1, :-2, 1:-1]
    beside = beside + field[1:-1, 1:-1, 2:] + field[1:-1, 1:-1, :-2]
    diagonal = 6.0 + shift_ext
    field = centre + relax_weight * (rhs_ext - (diagonal * centre - beside)) / diagonal
    return field


def shards(initial, right_side, shift_field):
    relaxed = initial
    for round_idx in range(SWEEPS):
        widened = extended(relaxed, (("gx", 0), ("gy", 1), ("gz", 2)), 1)
        relaxed = relax_margin(widened, right_side, shift_field)
    return relaxed


def solution(mesh):
    return jax.shard_map(
        shards,
        mesh=mesh,
        in_specs=(P("gx", "gy", "gz"), P("gx", "gy", "gz"), P("gx", "gy", "gz")),
        out_specs=P("gx", "gy", "gz"),
        check_vma=False,
    )
```

profile of v0, /device:TPU:0, one launch (start us, length us, event | category | flops | bytes accessed | tf_op | source)
XLA Modules:
  0.0 124.0 jit_solution(4652320961579662044)
XLA Ops:
  0.0 0.8 fusion.47
  0.8 4.0 %collective-permute-start = (f32[1,32,256]{2,0,1:T(1,128)S(1)}, f32[1,32,256]{2,0,1:T(1,128)S(1)}, u32[]{:S(2)}, u32[]{:S(2)}) collective-permute-start(f32[1,32,256]{2,0,1:T(1,128)S(1)} %copy.6), channel_id=1, source_target_pairs={{8,0},{16,8},{24,16},{0,24},{9,1},{17,9},{25,17},{1,25},{10,2},{18... | collective-permute-start | bytes 98312 | tf_op jit(solution)/shard_map/ppermute | solution.py:21
  4.9 2.8 %copy.16 = f32[64,32,256]{2,0,1:T(8,128)S(1)} copy(f32[64,32,256]{2,1,0:T(8,128)} %param.3) | data formatting | bytes 4194304 | tf_op args[0]
  7.7 2.0 %collective-permute-done.1 = f32[1,32,256]{2,0,1:T(1,128)S(1)} collective-permute-done((f32[1,32,256]{2,0,1:T(1,128)S(1)}, f32[1,32,256]{2,0,1:T(1,128)S(1)}, u32[]{:S(2)}, u32[]{:S(2)}) %collective-permute-start.1) | collective-permute-done | bytes 32800 | tf_op jit(solution)/shard_map/ppermute | solution.py:19
  10.3 0.8 collective-permute-done.3
  12.3 0.5 copy.11
  12.8 3.6 %collective-permute-start.4 = (f32[66,34,1]{0,1,2:T(8,128)S(1)}, f32[66,34,1]{0,1,2:T(8,128)S(1)}, u32[]{:S(2)}, u32[]{:S(2)}) collective-permute-start(f32[66,34,1]{0,1,2:T(8,128)S(1)} %copy.11), channel_id=1, source_target_pairs={{1,0},{2,1},{3,2},{0,3},{5,4},{6,5},{7,6},{4,7},{9,8},{10,9},{11,1... | collective-permute-start | bytes 26936 | tf_op jit(solution)/shard_map/ppermute | solution.py:21
  17.0 0.9 collective-permute-done.4
  17.9 0.6 copy.12
  18.5 4.1 %collective-permute-done.5 = f32[66,34,1]{0,1,2:T(8,128)S(1)} collective-permute-done((f32[66,34,1]{0,1,2:T(8,128)S(1)}, f32[66,34,1]{0,1,2:T(8,128)S(1)}, u32[]{:S(2)}, u32[]{:S(2)}) %collective-permute-start.5) | collective-permute-done | bytes 9008 | tf_op jit(solution)/shard_map/ppermute | solution.py:19
  22.6 1.6 %copy.14 = f32[66,34,1]{2,0,1:T(8,128)} copy(f32[66,34,1]{0,1,2:T(8,128)S(1)} %collective-permute-done.5) | data formatting | bytes 17952 | tf_op jit(solution)/shard_map/ppermute | solution.py:19
  24.1 14.4 %fusion.35 = f32[64,32,256]{2,0,1:T(8,128)S(1)} fusion(f32[64,32,256]{2,0,1:T(8,128)} %copy-done.4, f32[66,34,1]{2,0,1:T(8,128)} %copy.14, f32[66,1,256]{2,0,1:T(8,128)} %copy-done.5, f32[66,1,256]{2,0,1:T(8,128)S(1)} %collective-permute-done.3, f32[1,32,256]{2,0,1:T(1,128)S(1)} %collective-permute-done, f32[1,32,256]{2,0,1:T(1,128)S(1)} %collective-permute-done.1, ...), kind=kLoop, calls=%fused_computation.94 | loop fusion | flops 15728640 | bytes 8607264 | tf_op jit(solution)/shard_map/add | solution.py:34
  38.7 2.9 %collective-permute-start.6 = (f32[1,32,256]{2,0,1:T(1,128)S(1)}, f32[1,32,256]{2,0,1:T(1,128)S(1)}, u32[]{:S(2)}, u32[]{:S(2)}) collective-permute-start(f32[1,32,256]{2,0,1:T(1,128)S(1)} %get-tuple-element.26), channel_id=1, source_target_pairs={{8,0},{16,8},{24,16},{0,24},{9,1},{17,9},{25,17},{1,25},{10,2},{18... | collective-permute-start | bytes 98312 | tf_op jit(solution)/shard_map/ppermute | solution.py:21
  41.6 1.9 %collective-permute-done.7 = f32[1,32,256]{2,0,1:T(1,128)S(1)} collective-permute-done((f32[1,32,256]{2,0,1:T(1,128)S(1)}, f32[1,32,256]{2,0,1:T(1,128)S(1)}, u32[]{:S(2)}, u32[]{:S(2)}) %collective-permute-start.7) | collective-permute-done | bytes 32800 | tf_op jit(solution)/shard_map/ppermute | solution.py:19
  44.1 0.8 collective-permute-done.9
  45.0 0.6 copy-done.6
  45.9 1.4 %fusion.42 = (f32[66,34,1]{2,0,1:T(8,128)}, f32[66,34,1]{2,0,1:T(8,128)S(1)}) fusion(f32[66,34,256]{2,0,1:T(8,128)S(1)} %pad_maximum_fusion.1), kind=kLoop, calls=%fused_computation.131 | loop fusion | bytes 35904 | tf_op jit(solution)/shard_map/slice | solution.py:15
  47.4 1.8 %copy.17 = f32[66,34,1]{0,1,2:T(8,128)S(1)} copy(f32[66,34,1]{2,0,1:T(8,128)} %get-tuple-element.9) | data formatting | bytes 17952 | tf_op jit(solution)/shard_map/slice | solution.py:15
  49.9 2.1 %collective-permute-start.11 = (f32[66,34,1]{0,1,2:T(8,128)S(1)}, f32[66,34,1]{0,1,2:T(8,128)}, u32[]{:S(2)}, u32[]{:S(2)}) collective-permute-start(f32[66,34,1]{0,1,2:T(8,128)S(1)} %copy.19), channel_id=1, source_target_pairs={{0,1},{1,2},{2,3},{3,0},{4,5},{5,6},{6,7},{7,4},{8,9},{9,10},{10,1... | collective-permute-start | bytes 26936 | tf_op jit(solution)/shard_map/ppermute | solution.py:19
  52.0 1.0 collective-permute-done.10
  53.0 0.6 copy.18
  53.6 2.2 %collective-permute-done.11 = f32[66,34,1]{0,1,2:T(8,128)} collective-permute-done((f32[66,34,1]{0,1,2:T(8,128)S(1)}, f32[66,34,1]{0,1,2:T(8,128)}, u32[]{:S(2)}, u32[]{:S(2)}) %collective-permute-start.11) | collective-permute-done | bytes 9008 | tf_op jit(solution)/shard_map/ppermute | solution.py:19
  55.8 2.3 %copy.20 = f32[66,34,1]{2,0,1:T(8,128)} copy(f32[66,34,1]{0,1,2:T(8,128)} %collective-permute-done.11) | data formatting | bytes 17952 | tf_op jit(solution)/shard_map/ppermute | solution.py:19
  58.1 9.6 %fusion.25 = f32[64,32,256]{2,0,1:T(8,128)S(1)} fusion(f32[64,32,256]{2,0,1:T(8,128)S(1)} %fusion.35, f32[66,34,1]{2,0,1:T(8,128)} %copy.20, f32[66,1,256]{2,0,1:T(8,128)} %copy-done.6, f32[66,1,256]{2,0,1:T(8,128)S(1)} %collective-permute-done.9, f32[1,32,256]{2,0,1:T(1,128)S(1)} %collective-permute-done.6, f32[1,32,256]{2,0,1:T(1,128)S(1)} %collective-permute-done.7, ...), kind=kLoop, calls=%fused_computation.66 | loop fusion | flops 15728640 | bytes 8607264 | tf_op jit(solution)/shard_map/add | solution.py:34
  67.7 2.0 %collective-permute-start.13 = (f32[1,32,256]{2,0,1:T(1,128)S(1)}, f32[1,32,256]{2,0,1:T(1,128)S(1)}, u32[]{:S(2)}, u32[]{:S(2)}) collective-permute-start(f32[1,32,256]{2,0,1:T(1,128)S(1)} %get-tuple-element.23), channel_id=1, source_target_pairs={{0,8},{8,16},{16,24},{24,0},{1,9},{9,17},{17,25},{25,1},{2,10},{10... | collective-permute-start | bytes 98312 | tf_op jit(solution)/shard_map/ppermute | solution.py:19
  69.8 1.0 collective-permute-start.12
  70.8 2.0 %collective-permute-done.13 = f32[1,32,256]{2,0,1:T(1,128)S(1)} collective-permute-done((f32[1,32,256]{2,0,1:T(1,128)S(1)}, f32[1,32,256]{2,0,1:T(1,128)S(1)}, u32[]{:S(2)}, u32[]{:S(2)}) %collective-permute-start.13) | collective-permute-done | bytes 32800 | tf_op jit(solution)/shard_map/ppermute | solution.py:19
  72.8 0.9 collective-permute-done.12
  74.3 0.8 collective-permute-done.15
  76.2 0.5 copy.22
  76.8 0.5 copy.24
  77.3 2.0 %collective-permute-start.17 = (f32[66,34,1]{0,1,2:T(8,128)S(1)}, f32[66,34,1]{0,1,2:T(8,128)}, u32[]{:S(2)}, u32[]{:S(2)}) collective-permute-start(f32[66,34,1]{0,1,2:T(8,128)S(1)} %copy.24), channel_id=1, source_target_pairs={{0,1},{1,2},{2,3},{3,0},{4,5},{5,6},{6,7},{7,4},{8,9},{9,10},{10,1... | collective-permute-start | bytes 26936 | tf_op jit(solution)/shard_map/ppermute | solution.py:19
  79.3 1.2 collective-permute-done.16
  80.6 0.6 copy.23
  81.1 1.9 %collective-permute-done.17 = f32[66,34,1]{0,1,2:T(8,128)} collective-permute-done((f32[66,34,1]{0,1,2:T(8,128)S(1)}, f32[66,34,1]{0,1,2:T(8,128)}, u32[]{:S(2)}, u32[]{:S(2)}) %collective-permute-start.17) | collective-permute-done | bytes 9008 | tf_op jit(solution)/shard_map/ppermute | solution.py:19
  83.0 2.3 %copy.25 = f32[66,34,1]{2,0,1:T(8,128)} copy(f32[66,34,1]{0,1,2:T(8,128)} %collective-permute-done.17) | data formatting | bytes 17952 | tf_op jit(solution)/shard_map/ppermute | solution.py:19
  85.3 9.6 %fusion.15 = f32[64,32,256]{2,0,1:T(8,128)S(1)} fusion(f32[64,32,256]{2,0,1:T(8,128)S(1)} %copy-done.1, f32[66,34,1]{2,0,1:T(8,128)} %copy.25, f32[66,1,256]{2,0,1:T(8,128)} %copy-done.7, f32[66,1,256]{2,0,1:T(8,128)S(1)} %collective-permute-done.15, f32[1,32,256]{2,0,1:T(1,128)S(1)} %collective-permute-done.12, ...), kind=kLoop, calls=%fused_computation.38 | loop fusion | flops 15728640 | bytes 8607264 | tf_op jit(solution)/shard_map/add | solution.py:34
  95.0 1.4 %collective-permute-start.19 = (f32[1,32,256]{2,0,1:T(1,128)S(1)}, f32[1,32,256]{2,0,1:T(1,128)S(1)}, u32[]{:S(2)}, u32[]{:S(2)}) collective-permute-start(f32[1,32,256]{2,0,1:T(1,128)S(1)} %get-tuple-element.21), channel_id=1, source_target_pairs={{0,8},{8,16},{16,24},{24,0},{1,9},{9,17},{17,25},{25,1},{2,10},{10... | collective-permute-start | bytes 98312 | tf_op jit(solution)/shard_map/ppermute | solution.py:19
  96.3 1.6 %collective-permute-start.18 = (f32[1,32,256]{2,0,1:T(1,128)S(1)}, f32[1,32,256]{2,0,1:T(1,128)S(1)}, u32[]{:S(2)}, u32[]{:S(2)}) collective-permute-start(f32[1,32,256]{2,0,1:T(1,128)S(1)} %get-tuple-element.22), channel_id=1, source_target_pairs={{8,0},{16,8},{24,16},{0,24},{9,1},{17,9},{25,17},{1,25},{10,2},{18... | collective-permute-start | bytes 98312 | tf_op jit(solution)/shard_map/ppermute | solution.py:21
  98.0 1.9 %collective-permute-done.19 = f32[1,32,256]{2,0,1:T(1,128)S(1)} collective-permute-done((f32[1,32,256]{2,0,1:T(1,128)S(1)}, f32[1,32,256]{2,0,1:T(1,128)S(1)}, u32[]{:S(2)}, u32[]{:S(2)}) %collective-permute-start.19) | collective-permute-done | bytes 32800 | tf_op jit(solution)/shard_map/ppermute | solution.py:19
  100.9 0.8 collective-permute-done.21
  103.9 2.0 %collective-permute-start.23 = (f32[66,34,1]{0,1,2:T(8,128)S(1)}, f32[66,34,1]{0,1,2:T(8,128)}, u32[]{:S(2)}, u32[]{:S(2)}) collective-permute-start(f32[66,34,1]{0,1,2:T(8,128)S(1)} %copy.29), channel_id=1, source_target_pairs={{0,1},{1,2},{2,3},{3,0},{4,5},{5,6},{6,7},{7,4},{8,9},{9,10},{10,1... | collective-permute-start | bytes 26936 | tf_op jit(solution)/shard_map/ppermute | solution.py:19
  105.9 1.2 collective-permute-done.22
  107.2 0.6 copy.28
  107.7 1.9 %collective-permute-done.23 = f32[66,34,1]{0,1,2:T(8,128)} collective-permute-done((f32[66,34,1]{0,1,2:T(8,128)S(1)}, f32[66,34,1]{0,1,2:T(8,128)}, u32[]{:S(2)}, u32[]{:S(2)}) %collective-permute-start.23) | collective-permute-done | bytes 9008 | tf_op jit(solution)/shard_map/ppermute | solution.py:19
  109.6 2.3 %copy.30 = f32[66,34,1]{2,0,1:T(8,128)} copy(f32[66,34,1]{0,1,2:T(8,128)} %collective-permute-done.23) | data formatting | bytes 17952 | tf_op jit(solution)/shard_map/ppermute | solution.py:19
  111.9 9.6 %fusion.5 = f32[64,32,256]{2,0,1:T(8,128)S(1)} fusion(f32[64,32,256]{2,0,1:T(8,128)S(1)} %copy-done.3, f32[66,34,1]{2,0,1:T(8,128)} %copy.30, f32[66,1,256]{2,0,1:T(8,128)} %copy-done.8, f32[66,1,256]{2,0,1:T(8,128)S(1)} %collective-permute-done.21, f32[1,32,256]{2,0,1:T(1,128)S(1)} %collective-permute-done.18, ...), kind=kLoop, calls=%fused_computation.10 | loop fusion | flops 15728640 | bytes 8607264 | tf_op jit(solution)/shard_map/add | solution.py:34
  121.5 2.5 %copy.32 = f32[64,32,256]{2,1,0:T(8,128)} copy(f32[64,32,256]{2,0,1:T(8,128)S(1)} %fusion.5) | data formatting | bytes 4194304 | tf_op jit(solution)/shard_map/add | solution.py:34
  (58 shorter events, 9.5 us)
Async XLA Ops:
  0.8 6.9 %collective-permute-start = (f32[1,32,256]{2,0,1:T(1,128)S(1)}, f32[1,32,256]{2,0,1:T(1,128)S(1)}, u32[]{:S(2)}, u32[]{:S(2)}) collective-permute-start(f32[1,32,256]{2,0,1:T(1,128)S(1)} %copy.6), channel_id=1, source_target_pairs={{8,0},{16,8},{24,16},{0,24},{9,1},{17,9},{25,17},{1,25},{10,2},{18... | collective-permute-start | bytes 98312 | tf_op jit(solution)/shard_map/ppermute | solution.py:21
  4.8 4.9 %collective-permute-start.1 = (f32[1,32,256]{2,0,1:T(1,128)S(1)}, f32[1,32,256]{2,0,1:T(1,128)S(1)}, u32[]{:S(2)}, u32[]{:S(2)}) collective-permute-start(f32[1,32,256]{2,0,1:T(1,128)S(1)} %copy.8), channel_id=1, source_target_pairs={{0,8},{8,16},{16,24},{24,0},{1,9},{9,17},{17,25},{25,1},{2,10},{10... | collective-permute-start | bytes 98312 | tf_op jit(solution)/shard_map/ppermute | solution.py:19
  7.7 3.8 %copy-start.4 = (f32[64,32,256]{2,0,1:T(8,128)}, f32[64,32,256]{2,0,1:T(8,128)S(1)}, u32[]{:S(2)}) copy-start(f32[64,32,256]{2,0,1:T(8,128)S(1)} %copy.16) | copy-start | bytes 6291460
  9.7 1.3 %collective-permute-start.3 = (f32[66,1,256]{2,0,1:T(8,128)S(1)}, f32[66,1,256]{2,0,1:T(8,128)S(1)}, u32[]{:S(2)}, u32[]{:S(2)}) collective-permute-start(f32[66,1,256]{2,0,1:T(8,128)S(1)} %get-tuple-element.19), channel_id=1, source_target_pairs={{0,4},{4,0},{1,5},{5,1},{2,6},{6,2},{3,7},{7,3},{8,12},{12,8},{9,1... | collective-permute-start | bytes 202760 | tf_op jit(solution)/shard_map/ppermute | solution.py:19
  9.8 1.4 %collective-permute-start.2 = (f32[66,1,256]{2,0,1:T(8,128)S(1)}, f32[66,1,256]{2,0,1:T(8,128)S(1)}, u32[]{:S(2)}, u32[]{:S(2)}) collective-permute-start(f32[66,1,256]{2,0,1:T(8,128)S(1)} %get-tuple-element.20), channel_id=1, source_target_pairs={{4,0},{0,4},{5,1},{1,5},{6,2},{2,6},{7,3},{3,7},{12,8},{8,12},{13,... | collective-permute-start | bytes 202760 | tf_op jit(solution)/shard_map/ppermute | solution.py:21
  11.2 0.7 copy-start.5
  12.8 5.1 %collective-permute-start.4 = (f32[66,34,1]{0,1,2:T(8,128)S(1)}, f32[66,34,1]{0,1,2:T(8,128)S(1)}, u32[]{:S(2)}, u32[]{:S(2)}) collective-permute-start(f32[66,34,1]{0,1,2:T(8,128)S(1)} %copy.11), channel_id=1, source_target_pairs={{1,0},{2,1},{3,2},{0,3},{5,4},{6,5},{7,6},{4,7},{9,8},{10,9},{11,1... | collective-permute-start | bytes 26936 | tf_op jit(solution)/shard_map/ppermute | solution.py:21
  17.0 5.6 %collective-permute-start.5 = (f32[66,34,1]{0,1,2:T(8,128)S(1)}, f32[66,34,1]{0,1,2:T(8,128)S(1)}, u32[]{:S(2)}, u32[]{:S(2)}) collective-permute-start(f32[66,34,1]{0,1,2:T(8,128)S(1)} %copy.13), channel_id=1, source_target_pairs={{0,1},{1,2},{2,3},{3,0},{4,5},{5,6},{6,7},{7,4},{8,9},{9,10},{10,1... | collective-permute-start | bytes 26936 | tf_op jit(solution)/shard_map/ppermute | solution.py:19
  38.6 4.9 %collective-permute-start.7 = (f32[1,32,256]{2,0,1:T(1,128)S(1)}, f32[1,32,256]{2,0,1:T(1,128)S(1)}, u32[]{:S(2)}, u32[]{:S(2)}) collective-permute-start(f32[1,32,256]{2,0,1:T(1,128)S(1)} %get-tuple-element.25), channel_id=1, source_target_pairs={{0,8},{8,16},{16,24},{24,0},{1,9},{9,17},{17,25},{25,1},{2,10},{10... | collective-permute-start | bytes 98312 | tf_op jit(solution)/shard_map/ppermute | solution.py:19
  38.7 4.8 %collective-permute-start.6 = (f32[1,32,256]{2,0,1:T(1,128)S(1)}, f32[1,32,256]{2,0,1:T(1,128)S(1)}, u32[]{:S(2)}, u32[]{:S(2)}) collective-permute-start(f32[1,32,256]{2,0,1:T(1,128)S(1)} %get-tuple-element.26), channel_id=1, source_target_pairs={{8,0},{16,8},{24,16},{0,24},{9,1},{17,9},{25,17},{1,25},{10,2},{18... | collective-permute-start | bytes 98312 | tf_op jit(solution)/shard_map/ppermute | solution.py:21
  43.5 1.3 %collective-permute-start.9 = (f32[66,1,256]{2,0,1:T(8,128)S(1)}, f32[66,1,256]{2,0,1:T(8,128)S(1)}, u32[]{:S(2)}, u32[]{:S(2)}) collective-permute-start(f32[66,1,256]{2,0,1:T(8,128)S(1)} %get-tuple-element.17), channel_id=1, source_target_pairs={{0,4},{4,0},{1,5},{5,1},{2,6},{6,2},{3,7},{7,3},{8,12},{12,8},{9,1... | collective-permute-start | bytes 202760 | tf_op jit(solution)/shard_map/ppermute | solution.py:19
  43.6 1.4 %collective-permute-start.8 = (f32[66,1,256]{2,0,1:T(8,128)S(1)}, f32[66,1,256]{2,0,1:T(8,128)S(1)}, u32[]{:S(2)}, u32[]{:S(2)}) collective-permute-start(f32[66,1,256]{2,0,1:T(8,128)S(1)} %get-tuple-element.18), channel_id=1, source_target_pairs={{4,0},{0,4},{5,1},{1,5},{6,2},{2,6},{7,3},{3,7},{12,8},{8,12},{13,... | collective-permute-start | bytes 202760 | tf_op jit(solution)/shard_map/ppermute | solution.py:21
  45.0 0.6 copy-start.6
  49.2 3.8 %collective-permute-start.10 = (f32[66,34,1]{0,1,2:T(8,128)S(1)}, f32[66,34,1]{0,1,2:T(8,128)S(1)}, u32[]{:S(2)}, u32[]{:S(2)}) collective-permute-start(f32[66,34,1]{0,1,2:T(8,128)S(1)} %copy.17), channel_id=1, source_target_pairs={{1,0},{2,1},{3,2},{0,3},{5,4},{6,5},{7,6},{4,7},{9,8},{10,9},{11,1... | collective-permute-start | bytes 26936 | tf_op jit(solution)/shard_map/ppermute | solution.py:21
  49.9 5.9 %collective-permute-start.11 = (f32[66,34,1]{0,1,2:T(8,128)S(1)}, f32[66,34,1]{0,1,2:T(8,128)}, u32[]{:S(2)}, u32[]{:S(2)}) collective-permute-start(f32[66,34,1]{0,1,2:T(8,128)S(1)} %copy.19), channel_id=1, source_target_pairs={{0,1},{1,2},{2,3},{3,0},{4,5},{5,6},{6,7},{7,4},{8,9},{9,10},{10,1... | collective-permute-start | bytes 26936 | tf_op jit(solution)/shard_map/ppermute | solution.py:19
  67.7 7.8 %copy-start = (f32[64,32,256]{2,0,1:T(8,128)}, f32[64,32,256]{2,0,1:T(8,128)S(1)}, u32[]{:S(2)}) copy-start(f32[64,32,256]{2,0,1:T(8,128)S(1)} %fusion.25) | copy-start | bytes 6291460
  67.7 5.0 %collective-permute-start.13 = (f32[1,32,256]{2,0,1:T(1,128)S(1)}, f32[1,32,256]{2,0,1:T(1,128)S(1)}, u32[]{:S(2)}, u32[]{:S(2)}) collective-permute-start(f32[1,32,256]{2,0,1:T(1,128)S(1)} %get-tuple-element.23), channel_id=1, source_target_pairs={{0,8},{8,16},{16,24},{24,0},{1,9},{9,17},{17,25},{25,1},{2,10},{10... | collective-permute-start | bytes 98312 | tf_op jit(solution)/shard_map/ppermute | solution.py:19
  69.8 3.9 %collective-permute-start.12 = (f32[1,32,256]{2,0,1:T(1,128)S(1)}, f32[1,32,256]{2,0,1:T(1,128)S(1)}, u32[]{:S(2)}, u32[]{:S(2)}) collective-permute-start(f32[1,32,256]{2,0,1:T(1,128)S(1)} %get-tuple-element.24), channel_id=1, source_target_pairs={{8,0},{16,8},{24,16},{0,24},{9,1},{17,9},{25,17},{1,25},{10,2},{18... | collective-permute-start | bytes 98312 | tf_op jit(solution)/shard_map/ppermute | solution.py:21
  73.7 1.3 %collective-permute-start.15 = (f32[66,1,256]{2,0,1:T(8,128)S(1)}, f32[66,1,256]{2,0,1:T(8,128)S(1)}, u32[]{:S(2)}, u32[]{:S(2)}) collective-permute-start(f32[66,1,256]{2,0,1:T(8,128)S(1)} %get-tuple-element.15), channel_id=1, source_target_pairs={{0,4},{4,0},{1,5},{5,1},{2,6},{6,2},{3,7},{7,3},{8,12},{12,8},{9,1... | collective-permute-start | bytes 202760 | tf_op jit(solution)/shard_map/ppermute | solution.py:19
  73.8 1.4 %collective-permute-start.14 = (f32[66,1,256]{2,0,1:T(8,128)S(1)}, f32[66,1,256]{2,0,1:T(8,128)S(1)}, u32[]{:S(2)}, u32[]{:S(2)}) collective-permute-start(f32[66,1,256]{2,0,1:T(8,128)S(1)} %get-tuple-element.16), channel_id=1, source_target_pairs={{4,0},{0,4},{5,1},{1,5},{6,2},{2,6},{7,3},{3,7},{12,8},{8,12},{13,... | collective-permute-start | bytes 202760 | tf_op jit(solution)/shard_map/ppermute | solution.py:21
  75.2 0.6 copy-start.7
  76.7 8.6 %copy-start.1 = (f32[64,32,256]{2,0,1:T(8,128)S(1)}, f32[64,32,256]{2,0,1:T(8,128)}, u32[]{:S(2)}) copy-start(f32[64,32,256]{2,0,1:T(8,128)} %copy-done) | copy-start | bytes 6291460
  76.7 3.8 %collective-permute-start.16 = (f32[66,34,1]{0,1,2:T(8,128)S(1)}, f32[66,34,1]{0,1,2:T(8,128)S(1)}, u32[]{:S(2)}, u32[]{:S(2)}) collective-permute-start(f32[66,34,1]{0,1,2:T(8,128)S(1)} %copy.22), channel_id=1, source_target_pairs={{1,0},{2,1},{3,2},{0,3},{5,4},{6,5},{7,6},{4,7},{9,8},{10,9},{11,1... | collective-permute-start | bytes 26936 | tf_op jit(solution)/shard_map/ppermute | solution.py:21
  77.3 5.7 %collective-permute-start.17 = (f32[66,34,1]{0,1,2:T(8,128)S(1)}, f32[66,34,1]{0,1,2:T(8,128)}, u32[]{:S(2)}, u32[]{:S(2)}) collective-permute-start(f32[66,34,1]{0,1,2:T(8,128)S(1)} %copy.24), channel_id=1, source_target_pairs={{0,1},{1,2},{2,3},{3,0},{4,5},{5,6},{6,7},{7,4},{8,9},{9,10},{10,1... | collective-permute-start | bytes 26936 | tf_op jit(solution)/shard_map/ppermute | solution.py:19
  94.9 7.1 %copy-start.2 = (f32[64,32,256]{2,0,1:T(8,128)}, f32[64,32,256]{2,0,1:T(8,128)S(1)}, u32[]{:S(2)}) copy-start(f32[64,32,256]{2,0,1:T(8,128)S(1)} %fusion.15) | copy-start | bytes 6291460
  95.0 4.9 %collective-permute-start.19 = (f32[1,32,256]{2,0,1:T(1,128)S(1)}, f32[1,32,256]{2,0,1:T(1,128)S(1)}, u32[]{:S(2)}, u32[]{:S(2)}) collective-permute-start(f32[1,32,256]{2,0,1:T(1,128)S(1)} %get-tuple-element.21), channel_id=1, source_target_pairs={{0,8},{8,16},{16,24},{24,0},{1,9},{9,17},{17,25},{25,1},{2,10},{10... | collective-permute-start | bytes 98312 | tf_op jit(solution)/shard_map/ppermute | solution.py:19
  96.3 3.9 %collective-permute-start.18 = (f32[1,32,256]{2,0,1:T(1,128)S(1)}, f32[1,32,256]{2,0,1:T(1,128)S(1)}, u32[]{:S(2)}, u32[]{:S(2)}) collective-permute-start(f32[1,32,256]{2,0,1:T(1,128)S(1)} %get-tuple-element.22), channel_id=1, source_target_pairs={{8,0},{16,8},{24,16},{0,24},{9,1},{17,9},{25,17},{1,25},{10,2},{18... | collective-permute-start | bytes 98312 | tf_op jit(solution)/shard_map/ppermute | solution.py:21
  100.3 1.3 %collective-permute-start.21 = (f32[66,1,256]{2,0,1:T(8,128)S(1)}, f32[66,1,256]{2,0,1:T(8,128)S(1)}, u32[]{:S(2)}, u32[]{:S(2)}) collective-permute-start(f32[66,1,256]{2,0,1:T(8,128)S(1)} %get-tuple-element.13), channel_id=1, source_target_pairs={{0,4},{4,0},{1,5},{5,1},{2,6},{6,2},{3,7},{7,3},{8,12},{12,8},{9,1... | collective-permute-start | bytes 202760 | tf_op jit(solution)/shard_map/ppermute | solution.py:19
  100.4 1.4 %collective-permute-start.20 = (f32[66,1,256]{2,0,1:T(8,128)S(1)}, f32[66,1,256]{2,0,1:T(8,128)S(1)}, u32[]{:S(2)}, u32[]{:S(2)}) collective-permute-start(f32[66,1,256]{2,0,1:T(8,128)S(1)} %get-tuple-element.14), channel_id=1, source_target_pairs={{4,0},{0,4},{5,1},{1,5},{6,2},{2,6},{7,3},{3,7},{12,8},{8,12},{13,... | collective-permute-start | bytes 202760 | tf_op jit(solution)/shard_map/ppermute | solution.py:21
  101.8 0.6 copy-start.8
  103.3 8.6 %copy-start.3 = (f32[64,32,256]{2,0,1:T(8,128)S(1)}, f32[64,32,256]{2,0,1:T(8,128)}, u32[]{:S(2)}) copy-start(f32[64,32,256]{2,0,1:T(8,128)} %copy-done.2) | copy-start | bytes 6291460
  103.3 3.8 %collective-permute-start.22 = (f32[66,34,1]{0,1,2:T(8,128)S(1)}, f32[66,34,1]{0,1,2:T(8,128)S(1)}, u32[]{:S(2)}, u32[]{:S(2)}) collective-permute-start(f32[66,34,1]{0,1,2:T(8,128)S(1)} %copy.27), channel_id=1, source_target_pairs={{1,0},{2,1},{3,2},{0,3},{5,4},{6,5},{7,6},{4,7},{9,8},{10,9},{11,1... | collective-permute-start | bytes 26936 | tf_op jit(solution)/shard_map/ppermute | solution.py:21
  103.9 5.7 %collective-permute-start.23 = (f32[66,34,1]{0,1,2:T(8,128)S(1)}, f32[66,34,1]{0,1,2:T(8,128)}, u32[]{:S(2)}, u32[]{:S(2)}) collective-permute-start(f32[66,34,1]{0,1,2:T(8,128)S(1)} %copy.29), channel_id=1, source_target_pairs={{0,1},{1,2},{2,3},{3,0},{4,5},{5,6},{6,7},{7,4},{8,9},{9,10},{10,1... | collective-permute-start | bytes 26936 | tf_op jit(solution)/shard_map/ppermute | solution.py:19
where the time goes:
time: 124 us
  other arithmetic  44.4 us (36%)
  waiting for transfers between devices  27.2 us (22%)
  local copies, waits for them, and re-layouts  26.8 us (22%)
  starting transfers between devices  25.4 us (20%)
    add x4, other arithmetic, relax_margin(): centre + relax_weight * (rhs_ext - (diagonal * centre - beside)) / diagonal  43.3 us
    ppermute x12, waiting for transfers between devices, extended(): lax.ppermute(tail, axis, [(i, (i + 1) % count) for i in range(count)])  20.9 us
    ppermute x12, starting transfers between devices, extended(): lax.ppermute(head, axis, [((i + 1) % count, i) for i in range(count)])  15.4 us
    ppermute x12, starting transfers between devices, extended(): lax.ppermute(tail, axis, [(i, (i + 1) % count) for i in range(count)])  9.94 us
    ppermute x4, local copies, waits for them, and re-layouts, extended(): lax.ppermute(tail, axis, [(i, (i + 1) % count) for i in range(count)])  8.39 us
    ppermute x12, waiting for transfers between devices, extended(): lax.ppermute(head, axis, [((i + 1) % count, i) for i in range(count)])  6.3 us
    slice x9, local copies, waits for them, and re-layouts, extended(): head = lax.slice_in_dim(cells, 0, width, axis=dim)  6.01 us
    unnamed x19, local copies, waits for them, and re-layouts  4.58 us
  transfers between devices with their start and end apart: 24, of which 22 were waited for; matrix products, arithmetic and copies ran while one was open for 6% of the time, Pallas kernels for 0%

commit v1 on v0

v1 whole, which is shorter than its diff:
```python
import functools

import jax
import jax.numpy as jnp
import numpy as np
from jax import lax
from jax.experimental import pallas as pl
from jax.experimental.pallas import tpu as pltpu
from jax.sharding import PartitionSpec as P

SWEEPS = 4
WEIGHT = np.float32(0.8)
KEEP = np.float32(1.0) - WEIGHT
AXES = ("gx", "gy", "gz")
MESH = pl.DeviceIdType.MESH
ROWS = 8
LANES = 128


def beside(axis, step):
    count = lax.axis_size(axis)
    return {axis: lax.rem(lax.axis_index(axis) + (count + step), count)}


def iota(dim, shape):
    return lax.broadcasted_iota(jnp.int32, shape, dim)


def turned(block, shift, dim):
    size = block.shape[dim]
    shift = shift % size
    return block if shift == 0 else pltpu.roll(block, shift, dim)


def kernel(init_ref, rhs_ref, shift_ref, out_ref, v, q, w, ys, yh, zs, zh, load, send, recv):
    nx, ny, nz = out_ref.shape
    groups, bands, tiles = nx // ROWS, ny // ROWS, nz // LANES

    barrier = pltpu.get_barrier_semaphore()
    for axis in AXES:
        for step in (-1, 1):
            pl.semaphore_signal(barrier, inc=1, device_id=beside(axis, step), device_id_type=MESH)

    def init_copy(g):
        return pltpu.make_async_copy(
            init_ref.at[pl.ds(g * ROWS, ROWS)], v.at[0, pl.ds(g * ROWS + 1, ROWS)], load.at[g]
        )

    for g in range(groups):
        init_copy(g).start()
    rhs_copy = pltpu.make_async_copy(rhs_ref, q, load.at[groups])
    shift_copy = pltpu.make_async_copy(shift_ref, w, load.at[groups + 1])
    rhs_copy.start()
    shift_copy.start()

    def remote(src, dst, t, face, axis, step):
        return pltpu.make_async_remote_copy(
            src_ref=src,
            dst_ref=dst,
            send_sem=send.at[t, face],
            recv_sem=recv.at[t, face],
            device_id=beside(axis, step),
            device_id_type=MESH,
        )

    def x_copies(t):
        low = init_ref.at[0] if t == 0 else v.at[t, 1]
        high = init_ref.at[nx - 1] if t == 0 else v.at[t, nx]
        return (
            remote(high, v.at[t, 0], t, 0, "gx", 1),
            remote(low, v.at[t, nx + 1], t, 1, "gx", -1),
        )

    def z_copies(t):
        return (
            remote(zs.at[t, 1], zh.at[t, 0], t, 4, "gz", 1),
            remote(zs.at[t, 0], zh.at[t, 1], t, 5, "gz", -1),
        )

    def y_copies(t):
        return (
            remote(ys.at[t, 1], yh.at[t, 0], t, 2, "gy", 1),
            remote(ys.at[t, 0], yh.at[t, 1], t, 3, "gy", -1),
        )

    row = iota(0, (ROWS, nz))
    lane = iota(1, (ny, LANES))

    def pack(t, g, planes, carry):
        y_low, y_high = jnp.zeros((2, ROWS, nz), jnp.float32)
        z_low, z_high = jnp.zeros((2, ny, LANES), jnp.float32)
        for j, new in enumerate(planes):
            y_low = jnp.where(row == j, turned(new[:ROWS], j, 0), y_low)
            y_high = jnp.where(row == j, turned(new[ny - ROWS :], j + 1, 0), y_high)
            z_low = jnp.where(lane == j, turned(new[:, :LANES], j, 1), z_low)
            z_high = jnp.where(lane == j, turned(new[:, nz - LANES :], j + 1, 1), z_high)
        ys[t, 0, pl.ds(pl.multiple_of(g * ROWS, ROWS), ROWS)] = y_low
        ys[t, 1, pl.ds(pl.multiple_of(g * ROWS, ROWS), ROWS)] = y_high
        place = g * ROWS
        return (
            carry[0] + pltpu.roll(z_low, place, 1),
            carry[1] + pltpu.roll(z_high, place, 1),
        )

    def send_packed(t, carry):
        zs[t, 0] = carry[0]
        zs[t, 1] = carry[1]
        for copy in z_copies(t) + y_copies(t):
            copy.start()

    blank = (jnp.zeros((ny, LANES), jnp.float32), jnp.zeros((ny, LANES), jnp.float32))

    pl.semaphore_wait(barrier, 2 * len(AXES))
    for copy in x_copies(0):
        copy.start()

    def first_pack(g, carry):
        init_copy(g).wait()
        planes = [v[0, g * ROWS + 1 + j] for j in range(ROWS)]
        return pack(0, g, planes, carry)

    send_packed(0, lax.fori_loop(0, groups, first_pack, blank))

    rhs_copy.wait()
    shift_copy.wait()

    def prepare(x, carry):
        ratio = WEIGHT / (6.0 + w[x])
        w[x] = ratio
        q[x] = ratio * q[x]
        return carry

    lax.fori_loop(0, nx, prepare, 0)

    def relax_group(t, g, carry):
        base = g * ROWS
        aligned = pl.multiple_of(base, ROWS)
        y_low = yh[t, 0, pl.ds(aligned, ROWS)]
        y_high = yh[t, 1, pl.ds(aligned, ROWS)]
        back = lax.rem(LANES - base, LANES)
        z_low = pltpu.roll(zh[t, 0], back, 1)
        z_high = pltpu.roll(zh[t, 1], back, 1)
        planes = []
        for j in range(ROWS):
            c = v[t, base + 1 + j]
            total = v[t, base + j] + v[t, base + 2 + j]
            before = [turned(c[ROWS * k : ROWS * k + ROWS], 1, 0) for k in range(bands)]
            after = [turned(c[ROWS * k : ROWS * k + ROWS], -1, 0) for k in range(bands)]
            before_edge = [turned(y_low, -j, 0)] + before[:-1]
            after_edge = after[1:] + [turned(y_high, ROWS - 1 - j, 0)]
            total = total + jnp.concatenate(
                [
                    jnp.where(row == 0, before_edge[k], before[k])
                    + jnp.where(row == ROWS - 1, after_edge[k], after[k])
                    for k in range(bands)
                ],
                axis=0,
            )
            before = [turned(c[:, LANES * k : LANES * k + LANES], 1, 1) for k in range(tiles)]
            after = [turned(c[:, LANES * k : LANES * k + LANES], -1, 1) for k in range(tiles)]
            before_edge = [turned(z_low, -j, 1)] + before[:-1]
            after_edge = after[1:] + [turned(z_high, LANES - 1 - j, 1)]
            total = total + jnp.concatenate(
                [
                    jnp.where(lane == 0, before_edge[k], before[k])
                    + jnp.where(lane == LANES - 1, after_edge[k], after[k])
                    for k in range(tiles)
                ],
                axis=1,
            )
            new = (KEEP * c + q[base + j]) + w[base + j] * total
            if t + 1 < SWEEPS:
                v[t + 1, base + 1 + j] = new
                planes.append(new)
            else:
                out_ref[base + j] = new
        if t + 1 < SWEEPS:
            carry = pack(t + 1, g, planes, carry)
        return carry

    for t in range(SWEEPS):
        for copy in x_copies(t) + y_copies(t) + z_copies(t):
            copy.wait()
        body = functools.partial(relax_group, t)
        if t + 1 < SWEEPS:
            carry = lax.fori_loop(0, 2, lambda i, c: body(i * (groups - 1), c), blank)
            for copy in x_copies(t + 1):
                copy.start()
            send_packed(t + 1, lax.fori_loop(1, groups - 1, body, carry))
        else:
            lax.fori_loop(0, groups, body, 0)


def shards(initial, right_side, shift_field):
    nx, ny, nz = initial.shape
    assert nx % ROWS == 0 and 2 * ROWS <= nx <= LANES
    assert ny % ROWS == 0 and nz % LANES == 0
    faces = 2 * len(AXES)
    return pl.pallas_call(
        kernel,
        out_shape=pltpu.VMEM((nx, ny, nz), jnp.float32),
        in_specs=[pl.BlockSpec(memory_space=pltpu.HBM)] * 3,
        out_specs=pl.BlockSpec(memory_space=pltpu.VMEM),
        scratch_shapes=[
            pltpu.VMEM((SWEEPS, nx + 2, ny, nz), jnp.float32),
            pltpu.VMEM((nx, ny, nz), jnp.float32),
            pltpu.VMEM((nx, ny, nz), jnp.float32),
            pltpu.VMEM((SWEEPS, 2, nx, nz), jnp.float32),
            pltpu.VMEM((SWEEPS, 2, nx, nz), jnp.float32),
            pltpu.VMEM((SWEEPS, 2, ny, LANES), jnp.float32),
            pltpu.VMEM((SWEEPS, 2, ny, LANES), jnp.float32),
            pltpu.SemaphoreType.DMA((nx // ROWS + 2,)),
            pltpu.SemaphoreType.DMA((SWEEPS, faces)),
            pltpu.SemaphoreType.DMA((SWEEPS, faces)),
        ],
        compiler_params=pltpu.CompilerParams(
            collective_id=0, has_side_effects=True, vmem_limit_bytes=32 * 1024 * 1024
        ),
    )(*(pltpu.with_memory_space_constraint(a, pltpu.HBM) for a in (initial, right_side, shift_field)))


def solution(mesh):
    spec = P(*AXES)
    return jax.shard_map(
        shards, mesh=mesh, in_specs=(spec, spec, spec), out_specs=spec, check_vma=False
    )
```

time: 124 us -> 36.2 us (0.29)
  other arithmetic: 44.4 us -> 0 us
  Pallas kernels: 0 us -> 34.8 us
  waiting for transfers between devices: 27.2 us -> 0 us
  local copies, waits for them, and re-layouts: 26.8 us -> 1.32 us
  starting transfers between devices: 25.4 us -> 0 us
    add x4 -> x0, other arithmetic: 43.3 us -> none  [relax_margin(): centre + relax_weight * (rhs_ext - (diagonal * centre - beside)) / diagonal]
    pallas_call x0 -> x1, Pallas kernels: none -> 34.8 us  [shards(): pl.pallas_call(kernel, out_shape=pltpu.VMEM((nx, ny, nz), jnp.float32), i...]
    ppermute x24 -> x0, waiting for transfers between devices: 27.2 us -> none  [the longest x12 20.9 us: extended(): lax.ppermute(tail, axis, [(i, (i + 1) % count) for i in range(count)])]
    ppermute x24 -> x0, starting transfers between devices: 25.4 us -> none  [the longest x12 15.4 us: extended(): lax.ppermute(head, axis, [((i + 1) % count, i) for i in range(count)])]
    ppermute x8 -> x0, local copies, waits for them, and re-layouts: 10.6 us -> none  [the longest x4 8.39 us: extended(): lax.ppermute(tail, axis, [(i, (i + 1) % count) for i in range(count)])]
    slice x18 -> x0, local copies, waits for them, and re-layouts: 9.05 us -> none  [the longest x9 6.01 us: extended(): head = lax.slice_in_dim(cells, 0, width, axis=dim)]
    unnamed x19 -> x1, local copies, waits for them, and re-layouts: 4.58 us -> 1.32 us
    add x1 -> x0, local copies, waits for them, and re-layouts: 2.54 us -> none  [relax_margin(): centre + relax_weight * (rhs_ext - (diagonal * centre - beside)) / diagonal]
  transfers between devices with their start and end apart: 24 -> 0, of which waited for: 22 -> 0; matrix products, arithmetic and copies ran while one was open for 6% -> 0% of each run, Pallas kernels for 0% -> 0%
where the time goes in v1:
time: 36.2 us; the launch traced here: 36.1 us
  Pallas kernels  34.8 us (96%)
  local copies, waits for them, and re-layouts  1.32 us (4%)
    pallas_call x1, Pallas kernels, shards(): pl.pallas_call(kernel, out_shape=pltpu.VMEM((nx, ny, nz), jnp.float32), i...  34.8 us
    unnamed x1, local copies, waits for them, and re-layouts  1.32 us

profile of v1, /device:TPU:0, one launch (start us, length us, event | category | flops | bytes accessed | tf_op | source)
XLA Modules:
  0.0 36.1 jit_solution(9830596090572407311)
XLA Ops:
  0.0 34.8 %shard_map.37 = f32[64,32,256]{2,1,0:T(8,128)S(1)} custom-call(f32[64,32,256]{2,1,0:T(8,128)} %init_ref.1, f32[64,32,256]{2,1,0:T(8,128)} %rhs_ref.1, f32[64,32,256]{2,1,0:T(8,128)} %shift_ref.1), custom_call_target="tpu_custom_call" | custom-call | tf_op jit(solution)/shard_map/pallas_call | solution.py:199
  34.8 1.3 %copy.5 = f32[64,32,256]{2,1,0:T(8,128)} copy(f32[64,32,256]{2,1,0:T(8,128)S(1)} %shard_map.37) | data formatting | bytes 4194304

commit v2 on v1

v2 whole, which is shorter than its diff:
```python
import functools

import jax
import jax.numpy as jnp
import numpy as np
from jax import lax
from jax.experimental import pallas as pl
from jax.experimental.pallas import tpu as pltpu
from jax.sharding import PartitionSpec as P

SWEEPS = 4
WEIGHT = np.float32(0.8)
KEEP = np.float32(1.0) - WEIGHT
AXES = ("gx", "gy", "gz")
MESH = pl.DeviceIdType.MESH
ROWS = 8
LANES = 128


def beside(axis, step):
    count = lax.axis_size(axis)
    return {axis: lax.rem(lax.axis_index(axis) + (count + step), count)}


def iota(dim, shape):
    return lax.broadcasted_iota(jnp.int32, shape, dim)


def turned(block, shift, dim):
    size = block.shape[dim]
    shift = shift % size
    return block if shift == 0 else pltpu.roll(block, shift, dim)


def kernel(init_ref, rhs_ref, shift_ref, out_ref, v, q, w, ys, yh, zs, zh, zp, wz, load, send, recv):
    nx, ny, nz = out_ref.shape
    groups, bands, tiles = nx // ROWS, ny // ROWS, nz // LANES

    barrier = pltpu.get_barrier_semaphore()
    for axis in AXES:
        for step in (-1, 1):
            pl.semaphore_signal(barrier, inc=1, device_id=beside(axis, step), device_id_type=MESH)

    def init_copy(g):
        return pltpu.make_async_copy(
            init_ref.at[pl.ds(g * ROWS, ROWS)], v.at[0, pl.ds(g * ROWS + 1, ROWS)], load.at[g]
        )

    for g in range(groups):
        init_copy(g).start()
    rhs_copy = pltpu.make_async_copy(rhs_ref, q, load.at[groups])
    shift_copy = pltpu.make_async_copy(shift_ref, w, load.at[groups + 1])
    rhs_copy.start()
    shift_copy.start()

    def remote(src, dst, t, face, axis, step):
        return pltpu.make_async_remote_copy(
            src_ref=src,
            dst_ref=dst,
            send_sem=send.at[t, face],
            recv_sem=recv.at[t, face],
            device_id=beside(axis, step),
            device_id_type=MESH,
        )

    def x_copies(t):
        low = init_ref.at[0] if t == 0 else v.at[t, 1]
        high = init_ref.at[nx - 1] if t == 0 else v.at[t, nx]
        return (
            remote(high, v.at[t, 0], t, 0, "gx", 1),
            remote(low, v.at[t, nx + 1], t, 1, "gx", -1),
        )

    def z_copies(t):
        return (
            remote(zs.at[t, 1], zh.at[t, 0], t, 4, "gz", 1),
            remote(zs.at[t, 0], zh.at[t, 1], t, 5, "gz", -1),
        )

    def y_copies(t):
        return (
            remote(ys.at[t, 1], yh.at[t, 0], t, 2, "gy", 1),
            remote(ys.at[t, 0], yh.at[t, 1], t, 3, "gy", -1),
        )

    row = iota(0, (ROWS, nz))
    row1 = iota(0, (ROWS, LANES))
    lane = iota(1, (ny, LANES))
    lane1 = iota(1, (ROWS, LANES))

    def put(t, x, new):
        if t < SWEEPS:
            v[t, x + 1] = new
        else:
            out_ref[x] = new

    def get(t, x):
        return v[t, x + 1] if t < SWEEPS else out_ref[x]

    def pack_rows(t, g, planes):
        low, high = jnp.zeros((2, ROWS, nz), jnp.float32)
        for j, new in enumerate(planes):
            low = jnp.where(row == j, turned(new[:ROWS], j, 0), low)
            high = jnp.where(row == j, turned(new[ny - ROWS :], j + 1, 0), high)
        ys[t, 0, pl.ds(pl.multiple_of(g * ROWS, ROWS), ROWS)] = low
        ys[t, 1, pl.ds(pl.multiple_of(g * ROWS, ROWS), ROWS)] = high

    def pack_columns(g, planes, carry):
        low, high = jnp.zeros((2, ny, LANES), jnp.float32)
        for j, new in enumerate(planes):
            low = jnp.where(lane == j, turned(new[:, :LANES], j, 1), low)
            high = jnp.where(lane == j, turned(new[:, nz - LANES :], j + 1, 1), high)
        return carry[0] + pltpu.roll(low, g * ROWS, 1), carry[1] + pltpu.roll(high, g * ROWS, 1)

    def start(copies):
        for copy in copies:
            copy.start()

    def wait(copies):
        for copy in copies:
            copy.wait()

    blank = (jnp.zeros((ny, LANES), jnp.float32), jnp.zeros((ny, LANES), jnp.float32))

    pl.semaphore_wait(barrier, 2 * len(AXES))
    start(x_copies(0))

    def first_pack(g, carry):
        init_copy(g).wait()
        planes = [v[0, g * ROWS + 1 + j] for j in range(ROWS)]
        pack_rows(0, g, planes)
        return pack_columns(g, planes, carry)

    packed = lax.fori_loop(0, groups, first_pack, blank)
    zs[0, 0], zs[0, 1] = packed
    start(z_copies(0) + y_copies(0))

    rhs_copy.wait()
    shift_copy.wait()

    def prepare(g, carry):
        planes = []
        for j in range(ROWS):
            x = g * ROWS + j
            ratio = WEIGHT / (6.0 + w[x])
            w[x] = ratio
            q[x] = ratio * q[x]
            planes.append(ratio)
        return pack_columns(g, planes, carry)

    packed = lax.fori_loop(0, groups, prepare, blank)
    wz[0], wz[1] = packed

    def blend(t, x, k, y_low, y_high, z_low, z_high):
        at = slice(ROWS * k, ROWS * k + ROWS)
        c = v[t, x + 1, at]
        total = v[t, x, at] + v[t, x + 2, at]
        above = v[t, x + 1, ROWS * k - ROWS : ROWS * k] if k else None
        below = v[t, x + 1, ROWS * k + ROWS : ROWS * k + 2 * ROWS] if k + 1 < bands else None
        above = turned(above, 1, 0) if k else y_low
        below = turned(below, -1, 0) if k + 1 < bands else y_high
        total = total + jnp.where(row == 0, above, turned(c, 1, 0))
        total = total + jnp.where(row == ROWS - 1, below, turned(c, -1, 0))
        before = [turned(c[:, LANES * i : LANES * i + LANES], 1, 1) for i in range(tiles)]
        after = [turned(c[:, LANES * i : LANES * i + LANES], -1, 1) for i in range(tiles)]
        before_edge = [z_low] + before[:-1]
        after_edge = after[1:] + [z_high]
        total = total + jnp.concatenate(
            [
                jnp.where(lane1 == 0, before_edge[i], before[i])
                + jnp.where(lane1 == LANES - 1, after_edge[i], after[i])
                for i in range(tiles)
            ],
            axis=1,
        )
        return (KEEP * c + q[x, at]) + w[x, at] * total

    def bulk_group(t, ks, g, carry, first=0, last=ROWS):
        base = g * ROWS
        aligned = pl.multiple_of(base, ROWS)
        y_low = yh[t, 0, pl.ds(aligned, ROWS)] if 0 in ks else None
        y_high = yh[t, 1, pl.ds(aligned, ROWS)] if bands - 1 in ks else None
        none = jnp.zeros((ROWS, LANES), jnp.float32)
        low = [none for _ in ks]
        high = [none for _ in ks]
        for j in range(first, last):
            x = base + j
            for i, k in enumerate(ks):
                new = blend(
                    t,
                    x,
                    k,
                    turned(y_low, -j, 0) if k == 0 else None,
                    turned(y_high, ROWS - 1 - j, 0) if k == bands - 1 else None,
                    none,
                    none,
                )
                if t + 1 < SWEEPS:
                    v[t + 1, x + 1, ROWS * k : ROWS * k + ROWS] = new
                else:
                    out_ref[x, ROWS * k : ROWS * k + ROWS] = new
                low[i] = jnp.where(lane1 == j, turned(new[:, :LANES], j, 1), low[i])
                high[i] = jnp.where(lane1 == j, turned(new[:, nz - LANES :], j + 1, 1), high[i])
        return tuple(
            old + pltpu.roll(add, base, 1) for old, add in zip(carry, low + high)
        )

    def bulk(t, ks):
        none = jnp.zeros((ROWS, LANES), jnp.float32)
        carry = bulk_group(t, ks, 0, (none,) * (2 * len(ks)), first=1)
        carry = lax.fori_loop(1, groups - 1, functools.partial(bulk_group, t, ks), carry)
        carry = bulk_group(t, ks, groups - 1, carry, last=ROWS - 1)
        for i, k in enumerate(ks):
            zp[0, ROWS * k : ROWS * k + ROWS] = carry[i]
            zp[1, ROWS * k : ROWS * k + ROWS] = carry[len(ks) + i]

    def edge_plane(t, x):
        base = x // ROWS * ROWS
        j = x - base
        parts = []
        for k in range(bands):
            at = slice(ROWS * k, ROWS * k + ROWS)
            parts.append(
                blend(
                    t,
                    x,
                    k,
                    turned(yh[t, 0, base : base + ROWS], -j, 0),
                    turned(yh[t, 1, base : base + ROWS], ROWS - 1 - j, 0),
                    turned(zh[t, 0, at], -x, 1),
                    turned(zh[t, 1, at], LANES - 1 - x, 1),
                )
            )
        return jnp.concatenate(parts, axis=0)

    def mend_group(t, g, carry, first=0, last=ROWS):
        base = g * ROWS
        back = lax.rem(LANES - base, LANES)
        z_low = pltpu.roll(zs[t, 0], back, 1)
        z_high = pltpu.roll(zs[t, 1], back, 1)
        planes = []
        for j in range(ROWS):
            plane = get(t, base + j)
            if first <= j < last:
                parts = [plane[:, LANES * i : LANES * i + LANES] for i in range(tiles)]
                parts[0] = jnp.where(lane == 0, turned(z_low, -j, 1), parts[0])
                parts[-1] = jnp.where(lane == LANES - 1, turned(z_high, LANES - 1 - j, 1), parts[-1])
                plane = jnp.concatenate(parts, axis=1)
                put(t, base + j, plane)
            planes.append(plane)
        if t < SWEEPS:
            pack_rows(t, g, planes)
        return carry

    outer = tuple(sorted({0, bands - 1}))
    inner = tuple(range(1, bands - 1))
    for t in range(SWEEPS):
        if inner:
            bulk(t, inner)
        wait(y_copies(t))
        bulk(t, outer)
        wait(x_copies(t) + z_copies(t))
        first_plane, last_plane = edge_plane(t, 0), edge_plane(t, nx - 1)
        put(t + 1, 0, first_plane)
        put(t + 1, nx - 1, last_plane)
        if t + 1 < SWEEPS:
            start(x_copies(t + 1))
        for side, cut, turn in ((0, slice(0, LANES), 0), (1, slice(nz - LANES, nz), 1)):
            face = zp[side] + wz[side] * zh[t, side]
            face = jnp.where(lane == 0, turned(first_plane[:, cut], turn, 1), face)
            face = jnp.where(lane == nx - 1, turned(last_plane[:, cut], nx - 1 + turn, 1), face)
            zs[t + 1, side] = face
        if t + 1 < SWEEPS:
            start(z_copies(t + 1))
        mend_group(t + 1, 0, 0, first=1)
        lax.fori_loop(1, groups - 1, functools.partial(mend_group, t + 1), 0)
        mend_group(t + 1, groups - 1, 0, last=ROWS - 1)
        if t + 1 < SWEEPS:
            start(y_copies(t + 1))


def shards(initial, right_side, shift_field):
    nx, ny, nz = initial.shape
    assert nx % ROWS == 0 and 2 * ROWS <= nx <= LANES
    assert ny % ROWS == 0 and nz % LANES == 0
    faces = 2 * len(AXES)
    return pl.pallas_call(
        kernel,
        out_shape=pltpu.VMEM((nx, ny, nz), jnp.float32),
        in_specs=[pl.BlockSpec(memory_space=pltpu.HBM)] * 3,
        out_specs=pl.BlockSpec(memory_space=pltpu.VMEM),
        scratch_shapes=[
            pltpu.VMEM((SWEEPS, nx + 2, ny, nz), jnp.float32),
            pltpu.VMEM((nx, ny, nz), jnp.float32),
            pltpu.VMEM((nx, ny, nz), jnp.float32),
            pltpu.VMEM((SWEEPS, 2, nx, nz), jnp.float32),
            pltpu.VMEM((SWEEPS, 2, nx, nz), jnp.float32),
            pltpu.VMEM((SWEEPS + 1, 2, ny, LANES), jnp.float32),
            pltpu.VMEM((SWEEPS, 2, ny, LANES), jnp.float32),
            pltpu.VMEM((2, ny, LANES), jnp.float32),
            pltpu.VMEM((2, ny, LANES), jnp.float32),
            pltpu.SemaphoreType.DMA((nx // ROWS + 2,)),
            pltpu.SemaphoreType.DMA((SWEEPS, faces)),
            pltpu.SemaphoreType.DMA((SWEEPS, faces)),
        ],
        compiler_params=pltpu.CompilerParams(
            collective_id=0, has_side_effects=True, vmem_limit_bytes=32 * 1024 * 1024
        ),
    )(*(pltpu.with_memory_space_constraint(a, pltpu.HBM) for a in (initial, right_side, shift_field)))


def solution(mesh):
    spec = P(*AXES)
    return jax.shard_map(
        shards, mesh=mesh, in_specs=(spec, spec, spec), out_specs=spec, check_vma=False
    )
```

time: 36.2 us -> 34.2 us (0.945)
  Pallas kernels: 34.8 us -> 32.7 us
    pallas_call x1, Pallas kernels: 34.8 us -> 32.7 us  [shards(): pl.pallas_call(kernel, out_shape=pltpu.VMEM((nx, ny, nz), jnp.float32), i...]
where the time goes in v2:
time: 34.2 us; the launch traced here: 34 us
  Pallas kernels  32.7 us (96%)
  local copies, waits for them, and re-layouts  1.32 us (4%)
    pallas_call x1, Pallas kernels, shards(): pl.pallas_call(kernel, out_shape=pltpu.VMEM((nx, ny, nz), jnp.float32), i...  32.7 us
    unnamed x1, local copies, waits for them, and re-layouts  1.32 us

profile of v2, /device:TPU:0, one launch (start us, length us, event | category | flops | bytes accessed | tf_op | source)
XLA Modules:
  0.0 34.0 jit_solution(17670956541122752608)
XLA Ops:
  0.0 32.7 %shard_map.37 = f32[64,32,256]{2,1,0:T(8,128)S(1)} custom-call(f32[64,32,256]{2,1,0:T(8,128)} %init_ref.1, f32[64,32,256]{2,1,0:T(8,128)} %rhs_ref.1, f32[64,32,256]{2,1,0:T(8,128)} %shift_ref.1), custom_call_target="tpu_custom_call" | custom-call | tf_op jit(solution)/shard_map/pallas_call | solution.py:287
  32.7 1.3 %copy.5 = f32[64,32,256]{2,1,0:T(8,128)} copy(f32[64,32,256]{2,1,0:T(8,128)S(1)} %shard_map.37) | data formatting | bytes 4194304
